TPU v7x, 32 devices: a whole 2x2x4 slice. The times are simulated.
32 devices in a mesh: zero: 2 (over core), model: 16 (over z, y, x).
Axes of the slice: x: 2, y: 2, z: 4, core: 2. Of those that a mesh axis runs over, the one named last changes fastest.
Arguments:
- w_gate: float32 [5120, 13824], P('zero', 'model'), may hold values from -0.125 to 0.125
- first_gate: float32 [5120, 13824], P('zero', 'model'), may hold values from -0.078125 to 0.078125
- second_gate: float32 [5120, 13824], P('zero', 'model'), may hold values from -0.078125 to 0.078125
- w_up: float32 [5120, 13824], P('zero', 'model'), may hold values from -0.125 to 0.125
- first_up: float32 [5120, 13824], P('zero', 'model'), may hold values from -0.078125 to 0.078125
- second_up: float32 [5120, 13824], P('zero', 'model'), may hold values from -0.078125 to 0.078125
- norm_train: float32 [5120], P(('zero', 'model')), may hold values from 0.25 to 1.75
- norm_step: float32 [5120], P(('zero', 'model')), may hold values from -0.3 to 0.3
Outputs:
- ready_gate: bfloat16 [5120, 13824], P(None, 'model')
- ready_up: bfloat16 [5120, 13824], P(None, 'model')
- column_gate: float32 [13824], P('model')
- column_up: float32 [13824], P('model')
- serve_norm: bfloat16 [5120], replicated
- latest_gate: float32 [5120, 13824], P('zero', 'model')
- latest_up: float32 [5120, 13824], P('zero', 'model')
All inputs are finite; a program needn't handle non-finite values. Where the computation divides by a largest or mean magnitude, that divisor is 1e-20 or more.
Results may differ from a plain program's by a relative error of at most 0.001.
Values may be sent and summed in bfloat16 or wider, within the bound.
A program may use at most 192 MiB of HBM per device.

v0:
```python
import jax
import jax.numpy as jnp
from jax import lax
from jax.sharding import PartitionSpec as P

learn_rate = 0.25
hold_rate = 0.8


def local(w_gate, first_gate, second_gate, w_up, first_up, second_up, norm_train, norm_step):
    hold_gate = hold_rate * first_gate + second_gate
    latest_gate = w_gate - learn_rate * hold_gate
    hold_up = hold_rate * first_up + second_up
    latest_up = w_up - learn_rate * hold_up
    column_gate, column_up = lax.pmax(
        (jnp.max(jnp.abs(latest_gate), axis=0), jnp.max(jnp.abs(latest_up), axis=0)), "zero"
    )
    narrow_gate, narrow_up = (
        (latest_gate / column_gate).astype(jnp.bfloat16),
        (latest_up / column_up).astype(jnp.bfloat16),
    )
    ready_gate, ready_up = (
        lax.all_gather(narrow_gate, "zero", axis=0, tiled=True),
        lax.all_gather(narrow_up, "zero", axis=0, tiled=True),
    )
    serve_norm = lax.all_gather(
        (norm_train + norm_step).astype(jnp.bfloat16), ("zero", "model"), axis=0, tiled=True
    )
    return (ready_gate, ready_up, column_gate, column_up, serve_norm, latest_gate, latest_up)


def solution(mesh):
    return jax.shard_map(
        local,
        mesh=mesh,
        in_specs=(
            P("zero", "model"),
            P("zero", "model"),
            P("zero", "model"),
            P("zero", "model"),
            P("zero", "model"),
            P("zero", "model"),
            P(("zero", "model")),
            P(("zero", "model")),
        ),
        out_specs=(
            P(None, "model"),
            P(None, "model"),
            P("model"),
            P("model"),
            P(),
            P("zero", "model"),
            P("zero", "model"),
        ),
        check_vma=False,
    )
```

profile of v0, /device:TPU:0, one launch (start us, length us, event | category | flops | bytes accessed | tf_op | source)
XLA Modules:
  0.0 112.4 jit_solution(1038821842591484810)
XLA Ops:
  7.2 0.0 all-gather.5.cloned.1.call-start
  7.2 24.4 %abs_reduce_fusion = (f32[864]{0:T(1024)S(1)}, f32[2560,864]{0,1:T(8,128)}, f32[864]{0:T(1024)S(1)}, f32[2560,864]{0,1:T(8,128)}) fusion(f32[2560,864]{0,1:T(8,128)} %param.11, f32[2560,864]{0,1:T(8,128)} %param.13, f32[2560,864]{0,1:T(8,128)} %param.12, f32[2560,864]{0,1:T(8,128)} %param.8, f32[2560,864]{0,1:T(8,128)} %param.10, f32[2560,864]{0,1:T(8,128)} %param.9), kind=kLoop, calls=%fused_computation.1 | loop fusion | flops 26540352 | bytes 70785792 | tf_op jit(solution)/shard_map/reduce_max | solution.py:16
  31.6 2.6 %all-reduce.1 = (f32[864]{0:T(1024)S(1)}, f32[864]{0:T(1024)S(1)}) all-reduce(f32[864]{0:T(1024)S(1)} %get-tuple-element.13, f32[864]{0:T(1024)S(1)} %get-tuple-element.9), channel_id=1, replica_groups=mesh['zero'=2,'model'=16] {'zero'}, use_global_device_ids=true, to_apply=%region_1.0 | all-reduce | flops 1728 | bytes 13824 | tf_op jit(solution)/shard_map/pmax | solution.py:15
  34.2 0.0 copy-start.1
  34.2 0.0 copy-start
  34.2 6.8 %divide_convert_fusion = bf16[2560,864]{0,1:T(8,128)(2,1)} fusion(f32[2560,864]{0,1:T(8,128)} %get-tuple-element.28, f32[864]{0:T(1024)S(1)} %get-tuple-element.25), kind=kLoop, calls=%fused_computation | loop fusion | flops 4423680 | bytes 13274496 | tf_op jit(solution)/shard_map/convert_element_type | solution.py:20
  41.0 0.0 all-gather.5.cloned.1.call-update
  41.1 0.0 copy-done.1
  41.1 0.0 all-gather.3.cloned.1.call-start
  41.1 0.0 copy-done
  41.1 0.0 copy-start.2
  41.1 0.0 copy-start.3
  41.1 6.8 %divide_convert_fusion.1 = bf16[2560,864]{0,1:T(8,128)(2,1)} fusion(f32[2560,864]{0,1:T(8,128)} %get-tuple-element.27, f32[864]{0:T(1024)S(1)} %get-tuple-element.24), kind=kLoop, calls=%fused_computation.3 | loop fusion | flops 4423680 | bytes 13274496 | tf_op jit(solution)/shard_map/convert_element_type | solution.py:19
  48.0 0.0 all-gather.3.cloned.1.call-update
  48.0 0.0 copy-done.2
  48.0 0.0 copy-done.3
  48.0 0.2 dynamic-update-slice
  48.3 42.0 %all-reduce = bf16[5120]{0:T(1024)(128)(2,1)} all-reduce(bf16[5120]{0:T(1024)(128)(2,1)S(1)} %dynamic-update-slice), channel_id=1, replica_groups=mesh['zero'=2,'model'=16] {'zero','model'}, use_global_device_ids=true, to_apply=%add | all-reduce | flops 5120 | bytes 20480
  90.3 0.0 all-gather.5.cloned.1.call-done
  90.3 0.0 all-gather.3.cloned.1.call-done
  90.3 7.7 %copy.18 = bf16[5120,864]{0,1:T(8,128)(2,1)} copy(bf16[5120,864]{0,1:T(8,128)(2,1)} %all-gather.3.cloned.1.call-done) | data formatting | bytes 17694720
  97.9 7.7 %copy.19 = bf16[5120,864]{0,1:T(8,128)(2,1)} copy(bf16[5120,864]{0,1:T(8,128)(2,1)} %all-gather.5.cloned.1.call-done) | data formatting | bytes 17694720
  (2 shorter events, 0.0 us)
Async XLA Ops:
  7.2 83.1 %all-gather.5.cloned.1.call-start = ((), (), s32[]{:S(2)}) async-start(), calls=%async_computation.1 | async-start | bytes 13271040 | tf_op jit(solution)/shard_map/all_gather | solution.py:24
  34.2 6.8 %copy-start.1 = (f32[864]{0:T(1024)}, f32[864]{0:T(1024)S(1)}, u32[]{:S(2)}) copy-start(f32[864]{0:T(1024)S(1)} %get-tuple-element.25) | copy-start | bytes 10372
  34.2 6.9 %copy-start = (f32[864]{0:T(1024)}, f32[864]{0:T(1024)S(1)}, u32[]{:S(2)}) copy-start(f32[864]{0:T(1024)S(1)} %get-tuple-element.24) | copy-start | bytes 10372
  41.1 49.2 %all-gather.3.cloned.1.call-start = ((), (), s32[]{:S(2)}) async-start(), calls=%async_computation | async-start | bytes 13271040 | tf_op jit(solution)/shard_map/all_gather | solution.py:23
  41.1 6.9 %copy-start.2 = (f32[160]{0:T(256)S(1)}, f32[160]{0:T(256)}, u32[]{:S(2)}) copy-start(f32[160]{0:T(256)} %param.14) | copy-start | bytes 1924
  41.1 6.9 %copy-start.3 = (f32[160]{0:T(256)S(1)}, f32[160]{0:T(256)}, u32[]{:S(2)}) copy-start(f32[160]{0:T(256)} %param.15) | copy-start | bytes 1924
Sparse Core Ops, SparseCore 0:
  41.2 23.5 all-gather.4
  66.9 22.2 all-gather.2
where the time goes:
time: 113 us; the launch traced here: 112 us
  blocking collectives  44.6 us (39%)
  other arithmetic  38 us (34%)
  local copies, waits for them, and re-layouts  15.6 us (14%)
  between operations  14.1 us (12%)
    unnamed x1, blocking collectives  42 us
    reduce_max x1, other arithmetic, local(): jnp.max(jnp.abs(latest_up), axis=0)  24.4 us
    unnamed x12, local copies, waits for them, and re-layouts  15.6 us
    convert_element_type x1, other arithmetic, local(): (latest_gate / column_gate).astype(jnp.bfloat16)  6.81 us
    convert_element_type x1, other arithmetic, local(): (latest_up / column_up).astype(jnp.bfloat16)  6.8 us
    pmax x1, blocking collectives, local(): lax.pmax((jnp.max(jnp.abs(latest_gate), axis=0), jnp.max(jnp.abs(latest_u...  2.64 us
  transfers between devices with their start and end apart: 2, of which 0 were waited for; matrix products, arithmetic and copies ran while one was open for 6% of the time, Pallas kernels for 0%

commit v1 on v0

v1 whole, which is shorter than its diff:
```python
import functools

import jax
import jax.numpy as jnp
from jax import lax
from jax.experimental import pallas as pl
from jax.experimental.pallas import tpu as pltpu
from jax.sharding import PartitionSpec as P

learn_rate = 0.25
hold_rate = 0.8
LANES = 128
MESH = pl.DeviceIdType.MESH


def block_rows(rows, most):
    return max(k for k in range(16, most + 1, 16) if rows % k == 0)


def update_kernel(
    nz, nm, K, slots, lag,
    wg, fg, sg, wu, fu, su, norm_in,
    latest, ready, scale, norm_all,
    stage_f, stage_s, part, part_in,
    w_sem, f_sem, s_sem, part_send, part_recv, ready_send, ready_recv, norm_send, norm_recv,
):
    me = lax.axis_index("zero")
    col = lax.axis_index("model")
    n = nz * nm
    flat = me * nm + col
    rows, width = wg.shape
    nb = rows // K
    T = 2 * nb
    mine = pl.ds(pl.multiple_of(me * width, LANES), width)
    peers = [lax.rem(me + d, nz) for d in range(1, nz)]

    def copies(w, f, s, base, t):
        slot = lax.rem(t, slots)
        here = pl.ds(pl.multiple_of(base * K, 16), K)
        there = pl.ds(pl.multiple_of(t * K, 16), K)
        return (
            pltpu.make_async_copy(w.at[here], latest.at[there], w_sem.at[slot]),
            pltpu.make_async_copy(f.at[here], stage_f.at[slot], f_sem.at[slot]),
            pltpu.make_async_copy(s.at[here], stage_s.at[slot], s_sem.at[slot]),
        )

    def start(t):
        @pl.when(t < nb)
        def _():
            for c in copies(wg, fg, sg, t, t):
                c.start()

        @pl.when(t >= nb)
        def _():
            for c in copies(wu, fu, su, t - nb, t):
                c.start()

    def target(d):
        other = lax.rem(flat + d, n)
        return other // nm, lax.rem(other, nm)

    barrier = pltpu.get_barrier_semaphore()

    def greet(d, carry):
        pl.semaphore_signal(barrier, inc=1, device_id=target(d), device_id_type=MESH)
        return carry

    lax.fori_loop(1, n, greet, 0)
    for t in range(min(slots, T)):
        start(jnp.int32(t))
    norm_all[pl.ds(flat, 1)] = norm_in[...]
    pl.semaphore_wait(barrier, n - 1)

    def send_norm(d, carry):
        pltpu.make_async_remote_copy(
            src_ref=norm_in, dst_ref=norm_all.at[pl.ds(flat, 1)],
            send_sem=norm_send, recv_sem=norm_recv,
            device_id=target(d), device_id_type=MESH,
        ).start()
        return carry

    lax.fori_loop(1, n, send_norm, 0)

    def first_half(t):
        for c in copies(wg, fg, sg, 0, t):
            c.wait()
        slot = lax.rem(t, slots)
        for g in range(K // 8):
            r = pl.ds(pl.multiple_of(t * K + g * 8, 8), 8)
            hold = hold_rate * stage_f[slot, g * 8:(g + 1) * 8] + stage_s[slot, g * 8:(g + 1) * 8]
            new = latest[r, :] - learn_rate * hold
            latest[r, :] = new
            size = jnp.abs(new)
            most = size[:, :LANES]
            for i in range(1, width // LANES):
                most = jnp.maximum(most, size[:, i * LANES:(i + 1) * LANES])
            part[t, g * 8:(g + 1) * 8] = most

        @pl.when(t + slots < T)
        def _():
            start(t + slots)

        for i, peer in enumerate(peers):
            pltpu.make_async_remote_copy(
                src_ref=part.at[t], dst_ref=part_in.at[me, t],
                send_sem=part_send.at[i], recv_sem=part_recv.at[t, me],
                device_id={"zero": peer}, device_id_type=MESH,
            ).start()

    def second_half(u):
        most = part[u]
        for peer in peers:
            pltpu.make_async_copy(part_in.at[peer, u], part_in.at[peer, u], part_recv.at[u, peer]).wait()
            most = jnp.maximum(most, part_in[peer, u])
        most = jnp.max(most, axis=1, keepdims=True)
        there = pl.ds(pl.multiple_of(u * K, 16), K)
        scale[there, :] = jnp.broadcast_to(most, (K, LANES))
        inverse = 1.0 / most
        for g in range(K // 16):
            r = pl.ds(pl.multiple_of(u * K + g * 16, 16), 16)
            ready[r, mine] = (latest[r, :] * inverse[g * 16:(g + 1) * 16]).astype(jnp.bfloat16)
        for i, peer in enumerate(peers):
            pltpu.make_async_remote_copy(
                src_ref=ready.at[there, mine], dst_ref=ready.at[there, mine],
                send_sem=ready_send.at[i], recv_sem=ready_recv.at[me],
                device_id={"zero": peer}, device_id_type=MESH,
            ).start()

    def step(t, carry):
        first_half(t)

        @pl.when(t >= lag)
        def _():
            second_half(t - lag)

        return carry

    def last(u, carry):
        second_half(u)
        return carry

    lax.fori_loop(0, T, step, 0)
    lax.fori_loop(T - lag, T, last, 0)

    for i, peer in enumerate(peers):
        pltpu.make_async_copy(part, part, part_send.at[i]).wait()
        pltpu.make_async_copy(ready.at[:, mine], ready.at[:, mine], ready_send.at[i]).wait()
        theirs = pl.ds(pl.multiple_of(peer * width, LANES), width)
        pltpu.make_async_copy(ready.at[:, theirs], ready.at[:, theirs], ready_recv.at[peer]).wait()
    others = norm_all.at[pl.ds(0, n - 1)]
    pltpu.make_async_copy(others, others, norm_send).wait()
    pltpu.make_async_copy(others, others, norm_recv).wait()


def write_kernel(latest, ready, scale, ready_g, ready_u, latest_g, latest_u, column_g, column_u, sems):
    rows = latest_g.shape[0]
    copies = []
    for i, (src, dst) in enumerate(
        ((ready, ready_g), (ready, ready_u), (latest, latest_g), (latest, latest_u))
    ):
        c = pltpu.make_async_copy(src.at[pl.ds((i % 2) * rows, rows)], dst, sems.at[i])
        c.start()
        copies.append(c)
    for half, out in enumerate((column_g, column_u)):
        for first in range(0, rows, LANES):
            k = min(LANES, rows - first)
            tile = scale[half * rows + first:half * rows + first + k, :]
            diagonal = lax.broadcasted_iota(jnp.int32, (k, LANES), 0) == lax.broadcasted_iota(jnp.int32, (k, LANES), 1)
            line = jnp.sum(jnp.where(diagonal, tile, 0.0), axis=0, keepdims=True)
            out[:, first:first + k] = line[:, :k]
    for c in copies:
        c.wait()


def local(nz, nm, w_gate, first_gate, second_gate, w_up, first_up, second_up, norm_train, norm_step):
    n = nz * nm
    width, rows = w_gate.shape
    share = norm_train.shape[0]
    K = block_rows(rows, 48)
    T = 2 * rows // K
    slots = min(12, T)
    lag = 2
    norm_in = (norm_train + norm_step).reshape(1, 1, share)
    hbm = pl.BlockSpec(memory_space=pl.ANY)
    vmem = pl.BlockSpec(memory_space=pltpu.VMEM)
    latest, ready, scale, norm_all = pl.pallas_call(
        functools.partial(update_kernel, nz, nm, K, slots, lag),
        out_shape=(
            pltpu.VMEM((2 * rows, width), jnp.float32),
            pltpu.VMEM((2 * rows, nz * width), jnp.bfloat16),
            pltpu.VMEM((2 * rows, LANES), jnp.float32),
            pltpu.VMEM((n, 1, share), jnp.float32),
        ),
        in_specs=[hbm] * 6 + [vmem],
        out_specs=(vmem,) * 4,
        scratch_shapes=[
            pltpu.VMEM((slots, K, width), jnp.float32),
            pltpu.VMEM((slots, K, width), jnp.float32),
            pltpu.VMEM((T, K, LANES), jnp.float32),
            pltpu.VMEM((nz, T, K, LANES), jnp.float32),
            pltpu.SemaphoreType.DMA((slots,)),
            pltpu.SemaphoreType.DMA((slots,)),
            pltpu.SemaphoreType.DMA((slots,)),
            pltpu.SemaphoreType.DMA((max(nz - 1, 1),)),
            pltpu.SemaphoreType.DMA((T, nz)),
            pltpu.SemaphoreType.DMA((max(nz - 1, 1),)),
            pltpu.SemaphoreType.DMA((nz,)),
            pltpu.SemaphoreType.DMA,
            pltpu.SemaphoreType.DMA,
        ],
        compiler_params=pltpu.CompilerParams(
            collective_id=0, has_side_effects=True, vmem_limit_bytes=20 * 1024 * 1024
        ),
        name="update",
    )(w_gate.T, first_gate.T, second_gate.T, w_up.T, first_up.T, second_up.T, norm_in)
    ready_g, ready_u, latest_g, latest_u, column_g, column_u = pl.pallas_call(
        write_kernel,
        out_shape=(
            jax.ShapeDtypeStruct((rows, nz * width), jnp.bfloat16),
            jax.ShapeDtypeStruct((rows, nz * width), jnp.bfloat16),
            jax.ShapeDtypeStruct((rows, width), jnp.float32),
            jax.ShapeDtypeStruct((rows, width), jnp.float32),
            jax.ShapeDtypeStruct((1, rows), jnp.float32),
            jax.ShapeDtypeStruct((1, rows), jnp.float32),
        ),
        in_specs=[vmem] * 3,
        out_specs=(hbm,) * 4 + (vmem,) * 2,
        scratch_shapes=[pltpu.SemaphoreType.DMA((4,))],
        name="write",
    )(latest, ready, scale)
    serve_norm = norm_all.reshape(n * share).astype(jnp.bfloat16)
    return (
        ready_g.T, ready_u.T, column_g.reshape(rows), column_u.reshape(rows), serve_norm,
        latest_g.T, latest_u.T,
    )


def solution(mesh):
    whole, both = P("zero", "model"), P(("zero", "model"))
    return jax.shard_map(
        functools.partial(local, mesh.shape["zero"], mesh.shape["model"]),
        mesh=mesh,
        in_specs=(whole,) * 6 + (both,) * 2,
        out_specs=(
            P(None, "model"), P(None, "model"), P("model"), P("model"), P(), whole, whole,
        ),
        check_vma=False,
    )
```

time: 113 us -> 69.7 us (0.62)
  Pallas kernels: 0 us -> 51.1 us
  blocking collectives: 44.6 us -> 0 us
  other arithmetic: 38 us -> 3.93 us
  between operations: 14.1 us -> 0.66 us
  local copies, waits for them, and re-layouts: 15.6 us -> 13.7 us
    pallas_call x0 -> x2, Pallas kernels: none -> 51.1 us  [the longest x1 27.4 us: local(): pl.pallas_call(functools.partial(update_kernel, nz, nm, K, slots, lag), o...]
    unnamed x1 -> x0, blocking collectives: 42 us -> none
    reduce_max x1 -> x0, other arithmetic: 24.4 us -> none  [local(): jnp.max(jnp.abs(latest_up), axis=0)]
    convert_element_type x3 -> x1, other arithmetic: 13.6 us -> 0.09 us  [local(): serve_norm = norm_all.reshape(n * share).astype(jnp.bfloat16)]
    pmax x1 -> x0, blocking collectives: 2.64 us -> none  [local(): lax.pmax((jnp.max(jnp.abs(latest_gate), axis=0), jnp.max(jnp.abs(latest_u...]
    unnamed x12 -> x6, local copies, waits for them, and re-layouts: 15.6 us -> 13 us
    pallas_call x0 -> x2, other arithmetic: none -> 2.58 us  [local(): pl.pallas_call(write_kernel, out_shape=(jax.ShapeDtypeStruct((rows, nz *...]
    add x0 -> x1, other arithmetic: none -> 1.26 us  [local(): norm_in = (norm_train + norm_step).reshape(1, 1, share)]
  transfers between devices with their start and end apart: 2 -> 0, of which waited for: 0 -> 0; matrix products, arithmetic and copies ran while one was open for 6% -> 0% of each run, Pallas kernels for 0% -> 0%
where the time goes in v1:
time: 69.7 us; the launch traced here: 69.4 us
  Pallas kernels  51.1 us (73%)
  local copies, waits for them, and re-layouts  13.7 us (20%)
  other arithmetic  3.93 us (6%)
    pallas_call x1, Pallas kernels, local(): pl.pallas_call(functools.partial(update_kernel, nz, nm, K, slots, lag), o...  27.4 us
    pallas_call x1, Pallas kernels, local(): pl.pallas_call(write_kernel, out_shape=(jax.ShapeDtypeStruct((rows, nz *...  23.7 us
    unnamed x6, local copies, waits for them, and re-layouts  13 us
    pallas_call x2, other arithmetic, local(): pl.pallas_call(write_kernel, out_shape=(jax.ShapeDtypeStruct((rows, nz *...  2.58 us

profile of v1, /device:TPU:0, one launch (start us, length us, event | category | flops | bytes accessed | tf_op | source)
XLA Modules:
  0.0 69.4 jit_solution(14020369961633393916)
XLA Ops:
  0.6 1.3 %add.3 = f32[160]{0:T(256)} add(f32[160]{0:T(256)} %param.14, f32[160]{0:T(256)} %param.15) | non-fusion elementwise | flops 160 | bytes 1920 | tf_op jit(solution)/shard_map/add | solution.py:183
  1.9 27.4 %update.1 = (f32[1728,2560]{1,0:T(8,128)S(1)}, bf16[1728,5120]{1,0:T(8,128)(2,1)S(1)}, f32[1728,128]{1,0:T(8,128)S(1)}, f32[32,1,160]{2,1,0:T(1,128)S(1)}) custom-call(f32[864,2560]{1,0:T(8,128)} %bitcast.11, f32[864,2560]{1,0:T(8,128)} %bitcast.12, f32[864,2560]{1,0:T(8,128)} %bitcast.13, f32[864,2560]{1,0:T(8,128)} %bitcast.14, f32[864,2560]{1,0:T(8,128)} %bitcast.15, ...), custom_call_target="tpu_custom_call" | custom-call | tf_op jit(solution)/shard_map/update/pallas_call | solution.py:186
  29.3 0.0 copy-start
  29.4 6.0 %copy-done = f32[1728,2560]{1,0:T(8,128)} copy-done((f32[1728,2560]{1,0:T(8,128)}, f32[1728,2560]{1,0:T(8,128)S(1)}, u32[]{:S(2)}) %copy-start) | copy-done | bytes 17694744
  35.4 0.0 copy-start.1
  35.4 6.0 %copy-done.1 = bf16[1728,5120]{1,0:T(8,128)(2,1)} copy-done((bf16[1728,5120]{1,0:T(8,128)(2,1)}, bf16[1728,5120]{1,0:T(8,128)(2,1)S(1)}, u32[]{:S(2)}) %copy-start.1) | copy-done | bytes 17694744
  41.4 0.0 copy-start.2
  41.4 0.9 %copy-done.2 = f32[1728,128]{1,0:T(8,128)} copy-done((f32[1728,128]{1,0:T(8,128)}, f32[1728,128]{1,0:T(8,128)S(1)}, u32[]{:S(2)}) %copy-start.2) | copy-done | bytes 884760
  42.3 23.7 %write.1 = (bf16[864,5120]{1,0:T(8,128)(2,1)}, bf16[864,5120]{1,0:T(8,128)(2,1)}, f32[864,2560]{1,0:T(8,128)}, f32[864,2560]{1,0:T(8,128)}, f32[1,864]{1,0:T(1,128)}, /*index=5*/f32[1,864]{1,0:T(1,128)}) custom-call(f32[1728,2560]{1,0:T(8,128)} %copy-done, bf16[1728,5120]{1,0:T(8,128)(2,1)} %copy-done.1, f32[1728,128]{1,0:T(8,128)} %copy-done.2), custom_call_target="tpu_custom_call" | custom-call | tf_op jit(solution)/shard_map/write/pallas_call | solution.py:216
  66.0 1.3 %reduce = f32[864]{0:T(1024)} reduce(f32[1,864]{1,0:T(1,128)} %get-tuple-element.22, f32[]{:T(128)} %constant), dimensions={0}, to_apply=%get-tuple-element.22.reduce_sub_computation | reduce | bytes 6916 | tf_op jit(solution)/shard_map/write/pallas_call | solution.py:216
  67.3 1.3 %reduce.1 = f32[864]{0:T(1024)} reduce(f32[1,864]{1,0:T(1,128)} %get-tuple-element.23, f32[]{:T(128)} %constant), dimensions={0}, to_apply=%get-tuple-element.23.reduce_sub_computation | reduce | bytes 6916 | tf_op jit(solution)/shard_map/write/pallas_call | solution.py:216
  68.6 0.1 convert_reduce_fusion
  68.7 0.7 %convert_element_type.7 = bf16[5120]{0:T(1024)(128)(2,1)} reshape(bf16[32,160]{1,0:T(8,128)(2,1)S(1)} %convert_reduce_fusion) | data formatting | bytes 20480 | tf_op jit(solution)/shard_map/convert_element_type | solution.py:231
Async XLA Ops:
  29.3 6.1 %copy-start = (f32[1728,2560]{1,0:T(8,128)}, f32[1728,2560]{1,0:T(8,128)S(1)}, u32[]{:S(2)}) copy-start(f32[1728,2560]{1,0:T(8,128)S(1)} %get-tuple-element.17.latest) | copy-start | bytes 53084164
  35.4 6.0 %copy-start.1 = (bf16[1728,5120]{1,0:T(8,128)(2,1)}, bf16[1728,5120]{1,0:T(8,128)(2,1)S(1)}, u32[]{:S(2)}) copy-start(bf16[1728,5120]{1,0:T(8,128)(2,1)S(1)} %get-tuple-element.18.ready) | copy-start | bytes 53084164
  41.4 0.9 %copy-start.2 = (f32[1728,128]{1,0:T(8,128)}, f32[1728,128]{1,0:T(8,128)S(1)}, u32[]{:S(2)}) copy-start(f32[1728,128]{1,0:T(8,128)S(1)} %get-tuple-element.19.scale) | copy-start | bytes 2654212

commit v2 on v1

v2 whole, which is shorter than its diff:
```python
import functools

import jax
import jax.numpy as jnp
from jax import lax
from jax.experimental import pallas as pl
from jax.experimental.pallas import tpu as pltpu
from jax.sharding import PartitionSpec as P

learn_rate = 0.25
hold_rate = 0.8
LANES = 128
MESH = pl.DeviceIdType.MESH


def block_rows(rows, most):
    return max(k for k in range(16, most + 1, 16) if rows % k == 0)


def update_kernel(
    nz, nm, K, slots, lag,
    wg, fg, sg, wu, fu, su, norm_train, norm_step,
    ready_g, ready_u, column_g, column_u, latest_g, latest_u, serve_norm,
    stage_f, stage_s, part, part_in, scale, norm_all, norm_sum,
    w_sem, f_sem, s_sem, part_send, part_recv, ready_send, ready_recv, norm_send, norm_recv,
):
    me = lax.axis_index("zero")
    col = lax.axis_index("model")
    n = nz * nm
    flat = me * nm + col
    rows, width = wg.shape
    nb = rows // K
    T = 2 * nb
    mine = pl.ds(pl.multiple_of(me * width, LANES), width)
    peers = [lax.rem(me + d, nz) for d in range(1, nz)]
    gate = (wg, fg, sg, latest_g, ready_g, column_g, 0)
    up = (wu, fu, su, latest_u, ready_u, column_u, nb)

    def copies(side, t):
        w, f, s, latest, _, _, base = side
        slot = lax.rem(t, slots)
        here = pl.ds(pl.multiple_of((t - base) * K, 16), K)
        return (
            pltpu.make_async_copy(w.at[here], latest.at[here], w_sem.at[slot]),
            pltpu.make_async_copy(f.at[here], stage_f.at[slot], f_sem.at[slot]),
            pltpu.make_async_copy(s.at[here], stage_s.at[slot], s_sem.at[slot]),
        )

    def start(t):
        @pl.when(t < nb)
        def _():
            for c in copies(gate, t):
                c.start()

        @pl.when(t >= nb)
        def _():
            for c in copies(up, t):
                c.start()

    def target(d):
        other = lax.rem(flat + d, n)
        return other // nm, lax.rem(other, nm)

    barrier = pltpu.get_barrier_semaphore()

    for t in range(min(slots, T)):
        start(jnp.int32(t))

    def greet(d, carry):
        pl.semaphore_signal(barrier, inc=1, device_id=target(d), device_id_type=MESH)
        return carry

    lax.fori_loop(1, n, greet, 0)
    share = norm_train.shape[0]
    window = norm_all.shape[2]
    norm_all[flat] = jnp.zeros((1, window), jnp.float32)
    norm_all[flat, 0, 0:share] = norm_train[...] + norm_step[...]
    norm_all[flat] = pltpu.roll(norm_all[flat], lax.rem(flat * share, LANES), axis=1)
    pl.semaphore_wait(barrier, n - 1)

    def send_norm(d, carry):
        pltpu.make_async_remote_copy(
            src_ref=norm_all.at[flat], dst_ref=norm_all.at[flat],
            send_sem=norm_send, recv_sem=norm_recv,
            device_id=target(d), device_id_type=MESH,
        ).start()
        return carry

    lax.fori_loop(1, n, send_norm, 0)

    def first_half(side, t):
        latest, base = side[3], side[6]
        for c in copies(side, t):
            c.wait()
        slot = lax.rem(t, slots)
        for g in range(K // 8):
            r = pl.ds(pl.multiple_of((t - base) * K + g * 8, 8), 8)
            hold = hold_rate * stage_f[slot, g * 8:(g + 1) * 8] + stage_s[slot, g * 8:(g + 1) * 8]
            new = latest[r, :] - learn_rate * hold
            latest[r, :] = new
            size = jnp.abs(new)
            most = size[:, :LANES]
            for i in range(1, width // LANES):
                most = jnp.maximum(most, size[:, i * LANES:(i + 1) * LANES])
            part[t, g * 8:(g + 1) * 8] = most

        @pl.when(t + slots < T)
        def _():
            start(t + slots)

        for i, peer in enumerate(peers):
            pltpu.make_async_remote_copy(
                src_ref=part.at[t], dst_ref=part_in.at[me, t],
                send_sem=part_send.at[i], recv_sem=part_recv.at[t, me],
                device_id={"zero": peer}, device_id_type=MESH,
            ).start()

    def second_half(side, u):
        latest, ready, base = side[3], side[4], side[6]
        most = part[u]
        for peer in peers:
            pltpu.make_async_copy(part_in.at[peer, u], part_in.at[peer, u], part_recv.at[u, peer]).wait()
            most = jnp.maximum(most, part_in[peer, u])
        most = jnp.max(most, axis=1, keepdims=True)
        there = pl.ds(pl.multiple_of((u - base) * K, 16), K)
        scale[there, :] = jnp.broadcast_to(most, (K, LANES))
        inverse = 1.0 / most
        for g in range(K // 16):
            r = pl.ds(pl.multiple_of((u - base) * K + g * 16, 16), 16)
            ready[r, mine] = (latest[r, :] * inverse[g * 16:(g + 1) * 16]).astype(jnp.bfloat16)
        for i, peer in enumerate(peers):
            pltpu.make_async_remote_copy(
                src_ref=ready.at[there, mine], dst_ref=ready.at[there, mine],
                send_sem=ready_send.at[base // nb, i], recv_sem=ready_recv.at[base // nb, me],
                device_id={"zero": peer}, device_id_type=MESH,
            ).start()

    def columns(side):
        out = side[5]
        for first in range(0, rows, LANES):
            k = min(LANES, rows - first)
            tile = scale[first:first + k, :]
            diagonal = lax.broadcasted_iota(jnp.int32, (k, LANES), 0) == lax.broadcasted_iota(jnp.int32, (k, LANES), 1)
            line = jnp.sum(jnp.where(diagonal, tile, 0.0), axis=0)
            out[first:first + k] = line[:k]

    def run(low, high, ahead, behind):
        def step(t, carry):
            if ahead is not None:
                first_half(ahead, t)
            if behind is not None:
                second_half(behind, t - lag)
            return carry

        lax.fori_loop(low, high, step, 0)

    run(0, lag, gate, None)
    run(lag, nb, gate, gate)
    run(nb, nb + lag, up, gate)
    columns(gate)
    run(nb + lag, T, up, up)
    run(T, T + lag, None, up)
    columns(up)

    for i, peer in enumerate(peers):
        pltpu.make_async_copy(part, part, part_send.at[i]).wait()
        theirs = pl.ds(pl.multiple_of(peer * width, LANES), width)
        for half, ready in enumerate((ready_g, ready_u)):
            pltpu.make_async_copy(ready.at[:, mine], ready.at[:, mine], ready_send.at[half, i]).wait()
            pltpu.make_async_copy(ready.at[:, theirs], ready.at[:, theirs], ready_recv.at[half, peer]).wait()
    others = norm_all.at[pl.ds(0, n - 1)]
    pltpu.make_async_copy(others, others, norm_send).wait()
    pltpu.make_async_copy(others, others, norm_recv).wait()
    norm_sum[...] = jnp.zeros_like(norm_sum)
    for d in range(n):
        first = d * share // LANES * LANES
        norm_sum[:, first:first + window] += norm_all[d]
    serve_norm[...] = norm_sum[0, :n * share].astype(jnp.bfloat16)


def copy_kernel(*refs):
    sems = refs[8]
    copies = [pltpu.make_async_copy(refs[i], refs[4 + i], sems.at[i]) for i in range(4)]
    for c in copies:
        c.start()
    for c in copies:
        c.wait()


def local(nz, nm, w_gate, first_gate, second_gate, w_up, first_up, second_up, norm_train, norm_step):
    n = nz * nm
    width, rows = w_gate.shape
    share = norm_train.shape[0]
    K = block_rows(rows, 48)
    T = 2 * rows // K
    slots = min(8, T)
    lag = 2
    window = -(-(share + LANES - 1) // LANES) * LANES
    hbm = pl.BlockSpec(memory_space=pl.ANY)
    vmem = pl.BlockSpec(memory_space=pltpu.VMEM)
    ready_g, ready_u, column_g, column_u, latest_g, latest_u, serve_norm = pl.pallas_call(
        functools.partial(update_kernel, nz, nm, K, slots, lag),
        out_shape=(
            pltpu.VMEM((rows, nz * width), jnp.bfloat16),
            pltpu.VMEM((rows, nz * width), jnp.bfloat16),
            pltpu.VMEM((rows,), jnp.float32),
            pltpu.VMEM((rows,), jnp.float32),
            pltpu.VMEM((rows, width), jnp.float32),
            pltpu.VMEM((rows, width), jnp.float32),
            pltpu.VMEM((n * share,), jnp.bfloat16),
        ),
        in_specs=[hbm] * 6 + [vmem] * 2,
        out_specs=(vmem,) * 7,
        scratch_shapes=[
            pltpu.VMEM((slots, K, width), jnp.float32),
            pltpu.VMEM((slots, K, width), jnp.float32),
            pltpu.VMEM((T, K, LANES), jnp.float32),
            pltpu.VMEM((nz, T, K, LANES), jnp.float32),
            pltpu.VMEM((rows, LANES), jnp.float32),
            pltpu.VMEM((n, 1, window), jnp.float32),
            pltpu.VMEM((1, n * share + window), jnp.float32),
            pltpu.SemaphoreType.DMA((slots,)),
            pltpu.SemaphoreType.DMA((slots,)),
            pltpu.SemaphoreType.DMA((slots,)),
            pltpu.SemaphoreType.DMA((max(nz - 1, 1),)),
            pltpu.SemaphoreType.DMA((T, nz)),
            pltpu.SemaphoreType.DMA((2, max(nz - 1, 1))),
            pltpu.SemaphoreType.DMA((2, nz)),
            pltpu.SemaphoreType.DMA,
            pltpu.SemaphoreType.DMA,
        ],
        compiler_params=pltpu.CompilerParams(
            collective_id=0, has_side_effects=True, vmem_limit_bytes=12 * 1024 * 1024
        ),
        name="update",
    )(w_gate.T, first_gate.T, second_gate.T, w_up.T, first_up.T, second_up.T, norm_train, norm_step)
    ready_g, ready_u, latest_g, latest_u = pl.pallas_call(
        copy_kernel,
        out_shape=tuple(jax.ShapeDtypeStruct(x.shape, x.dtype) for x in (ready_g, ready_u, latest_g, latest_u)),
        in_specs=[hbm] * 4,
        out_specs=(hbm,) * 4,
        scratch_shapes=[pltpu.SemaphoreType.DMA((4,))],
        compiler_params=pltpu.CompilerParams(vmem_limit_bytes=1024 * 1024),
        name="write",
    )(ready_g, ready_u, latest_g, latest_u)
    return (ready_g.T, ready_u.T, column_g, column_u, serve_norm, latest_g.T, latest_u.T)


def solution(mesh):
    whole, both = P("zero", "model"), P(("zero", "model"))
    return jax.shard_map(
        functools.partial(local, mesh.shape["zero"], mesh.shape["model"]),
        mesh=mesh,
        in_specs=(whole,) * 6 + (both,) * 2,
        out_specs=(
            P(None, "model"), P(None, "model"), P("model"), P("model"), P(), whole, whole,
        ),
        check_vma=False,
    )
```

time: 69.7 us -> 43.1 us (0.62)
  Pallas kernels: 51.1 us -> 39.1 us
  local copies, waits for them, and re-layouts: 13.7 us -> 3.14 us
  other arithmetic: 3.93 us -> 0 us
    pallas_call x1, Pallas kernels: 23.7 us -> 11.8 us  [local(): pl.pallas_call(copy_kernel, out_shape=tuple((jax.ShapeDtypeStruct(x.shape...]
    unnamed x6 -> x7, local copies, waits for them, and re-layouts: 13 us -> 3.14 us
    pallas_call x2 -> x0, other arithmetic: 2.58 us -> none  [local(): pl.pallas_call(write_kernel, out_shape=(jax.ShapeDtypeStruct((rows, nz *...]
    add x1 -> x0, other arithmetic: 1.26 us -> none  [local(): norm_in = (norm_train + norm_step).reshape(1, 1, share)]
where the time goes in v2:
time: 43.1 us; the launch traced here: 42.9 us
  Pallas kernels  39.1 us (91%)
  local copies, waits for them, and re-layouts  3.14 us (7%)
  between operations  0.66 us (2%)
    pallas_call x1, Pallas kernels, local(): pl.pallas_call(functools.partial(update_kernel, nz, nm, K, slots, lag), o...  27.3 us
    pallas_call x1, Pallas kernels, local(): pl.pallas_call(copy_kernel, out_shape=tuple((jax.ShapeDtypeStruct(x.shape...  11.8 us
    unnamed x7, local copies, waits for them, and re-layouts  3.14 us

profile of v2, /device:TPU:0, one launch (start us, length us, event | category | flops | bytes accessed | tf_op | source)
XLA Modules:
  0.0 42.9 jit_solution(16741584388975871009)
XLA Ops:
  0.6 0.0 copy-start
  0.6 0.7 %copy-done = f32[160]{0:T(256)S(1)} copy-done((f32[160]{0:T(256)S(1)}, f32[160]{0:T(256)}, u32[]{:S(2)}) %copy-start) | copy-done | bytes 664
  1.3 0.0 copy-start.1
  1.3 0.7 %copy-done.1 = f32[160]{0:T(256)S(1)} copy-done((f32[160]{0:T(256)S(1)}, f32[160]{0:T(256)}, u32[]{:S(2)}) %copy-start.1) | copy-done | bytes 664
  2.0 27.3 %update.1 = (bf16[864,5120]{1,0:T(8,128)(2,1)S(1)}, bf16[864,5120]{1,0:T(8,128)(2,1)S(1)}, f32[864]{0:T(1024)S(1)}, f32[864]{0:T(1024)S(1)}, f32[864,2560]{1,0:T...) custom-call(f32[864,2560]{1,0:T(8,128)} %bitcast.10, f32[864,2560]{1,0:T(8,128)} %bitcast.11, ...), custom_call_target="tpu_custom_call" | custom-call | tf_op jit(solution)/shard_map/update/pallas_call | solution.py:201
  29.3 11.8 %write.1 = (bf16[864,5120]{1,0:T(8,128)(2,1)}, bf16[864,5120]{1,0:T(8,128)(2,1)}, f32[864,2560]{1,0:T(8,128)}, f32[864,2560]{1,0:T(8,128)}) custom-call(bf16[864,5120]{1,0:T(8,128)(2,1)S(1)} %get-tuple-element.18.refs_0_, bf16[864,5120]{1,0:T(8,128)(2,1)S(1)} %get-tuple-element.19.refs_1_, f32[864,2560]{1,0:T(8,128)S(1)} %get-tuple-element.20.refs_2_, ...), custom_call_target="tpu_custom_call" | custom-call | tf_op jit(solution)/shard_map/write/pallas_call | solution.py:237
  41.1 0.6 %copy.18 = f32[864]{0:T(1024)} copy(f32[864]{0:T(1024)S(1)} %get-tuple-element.31) | data formatting | bytes 6912
  41.7 0.6 %copy.19 = f32[864]{0:T(1024)} copy(f32[864]{0:T(1024)S(1)} %get-tuple-element.32) | data formatting | bytes 6912
  42.3 0.6 %copy.20 = bf16[5120]{0:T(1024)(128)(2,1)} copy(bf16[5120]{0:T(1024)(128)(2,1)S(1)} %get-tuple-element.33) | data formatting | bytes 20480
Async XLA Ops:
  0.6 0.7 %copy-start = (f32[160]{0:T(256)S(1)}, f32[160]{0:T(256)}, u32[]{:S(2)}) copy-start(f32[160]{0:T(256)} %norm_train.1) | copy-start | bytes 1924
  1.3 0.7 %copy-start.1 = (f32[160]{0:T(256)S(1)}, f32[160]{0:T(256)}, u32[]{:S(2)}) copy-start(f32[160]{0:T(256)} %norm_step.1) | copy-start | bytes 1924

commit v3 on v2

--- a/solution.py
+++ b/solution.py
@@ -18,11 +18,11 @@
 
 
 def update_kernel(
-    nz, nm, K, slots, lag,
+    nz, nm, K, slots, lag, quiet,
     wg, fg, sg, wu, fu, su, norm_train, norm_step,
     ready_g, ready_u, column_g, column_u, latest_g, latest_u, serve_norm,
-    stage_f, stage_s, part, part_in, scale, norm_all, norm_sum,
-    w_sem, f_sem, s_sem, part_send, part_recv, ready_send, ready_recv, norm_send, norm_recv,
+    stage_f, stage_s, part, part_in, scale, norm_all, norm_sum, norm_a, norm_b,
+    w_sem, f_sem, s_sem, part_send, part_recv, ready_send, ready_recv, norm_send, norm_recv, early_recv, norm_sem,
 ):
     me = lax.axis_index("zero")
     col = lax.axis_index("model")
@@ -63,6 +63,12 @@
 
     barrier = pltpu.get_barrier_semaphore()
 
+    norm_copies = (
+        pltpu.make_async_copy(norm_train, norm_a, norm_sem.at[0]),
+        pltpu.make_async_copy(norm_step, norm_b, norm_sem.at[1]),
+    )
+    for c in norm_copies:
+        c.start()
     for t in range(min(slots, T)):
         start(jnp.int32(t))
 
@@ -74,19 +80,6 @@
     share = norm_train.shape[0]
     window = norm_all.shape[2]
     norm_all[flat] = jnp.zeros((1, window), jnp.float32)
-    norm_all[flat, 0, 0:share] = norm_train[...] + norm_step[...]
-    norm_all[flat] = pltpu.roll(norm_all[flat], lax.rem(flat * share, LANES), axis=1)
-    pl.semaphore_wait(barrier, n - 1)
-
-    def send_norm(d, carry):
-        pltpu.make_async_remote_copy(
-            src_ref=norm_all.at[flat], dst_ref=norm_all.at[flat],
-            send_sem=norm_send, recv_sem=norm_recv,
-            device_id=target(d), device_id_type=MESH,
-        ).start()
-        return carry
-
-    lax.fori_loop(1, n, send_norm, 0)
 
     def first_half(side, t):
         latest, base = side[3], side[6]
@@ -108,22 +101,18 @@
         def _():
             start(t + slots)
 
-        for i, peer in enumerate(peers):
-            pltpu.make_async_remote_copy(
-                src_ref=part.at[t], dst_ref=part_in.at[me, t],
-                send_sem=part_send.at[i], recv_sem=part_recv.at[t, me],
-                device_id={"zero": peer}, device_id_type=MESH,
-            ).start()
-
     def second_half(side, u):
         latest, ready, base = side[3], side[4], side[6]
         most = part[u]
         for peer in peers:
-            pltpu.make_async_copy(part_in.at[peer, u], part_in.at[peer, u], part_recv.at[u, peer]).wait()
+            @pl.when(u >= quiet)
+            def _():
+                pltpu.make_async_copy(part_in.at[peer, u], part_in.at[peer, u], part_recv.at[u, peer]).wait()
+
             most = jnp.maximum(most, part_in[peer, u])
         most = jnp.max(most, axis=1, keepdims=True)
         there = pl.ds(pl.multiple_of((u - base) * K, 16), K)
-        scale[there, :] = jnp.broadcast_to(most, (K, LANES))
+        scale[pl.ds(pl.multiple_of(u * K, 16), K), :] = jnp.broadcast_to(most, (K, LANES))
         inverse = 1.0 / most
         for g in range(K // 16):
             r = pl.ds(pl.multiple_of((u - base) * K + g * 16, 16), 16)
@@ -139,35 +128,86 @@
         out = side[5]
         for first in range(0, rows, LANES):
             k = min(LANES, rows - first)
-            tile = scale[first:first + k, :]
+            tile = scale[side[6] * K + first:side[6] * K + first + k, :]
             diagonal = lax.broadcasted_iota(jnp.int32, (k, LANES), 0) == lax.broadcasted_iota(jnp.int32, (k, LANES), 1)
             line = jnp.sum(jnp.where(diagonal, tile, 0.0), axis=0)
             out[first:first + k] = line[:k]
 
-    def run(low, high, ahead, behind):
-        def step(t, carry):
-            if ahead is not None:
-                first_half(ahead, t)
-            if behind is not None:
-                second_half(behind, t - lag)
-            return carry
-
-        lax.fori_loop(low, high, step, 0)
-
-    run(0, lag, gate, None)
-    run(lag, nb, gate, gate)
-    run(nb, nb + lag, up, gate)
+    def ahead(t):
+        @pl.when(t < nb)
+        def _():
+            first_half(gate, t)
+
+        @pl.when(t >= nb)
+        def _():
+            first_half(up, t)
+
+    def behind(u):
+        @pl.when(u < nb)
+        def _():
+            second_half(gate, u)
+
+        @pl.when(u >= nb)
+        def _():
+            second_half(up, u)
+
+    def send_part(t):
+        for i, peer in enumerate(peers):
+            pltpu.make_async_remote_copy(
+                src_ref=part.at[t], dst_ref=part_in.at[me, t],
+                send_sem=part_send.at[i], recv_sem=part_recv.at[t, me],
+                device_id={"zero": peer}, device_id_type=MESH,
+            ).start()
+
+    def alone(t, carry):
+        ahead(t)
+        return carry
+
+    def catch_up(i, carry):
+        ahead(quiet + i)
+        send_part(quiet + i)
+        behind(2 * i)
+        behind(2 * i + 1)
+        return carry
+
+    def steady(t, carry):
+        ahead(t)
+        send_part(t)
+        behind(t - lag)
+        return carry
+
+    def last(u, carry):
+        behind(u)
+        return carry
+
+    lax.fori_loop(0, quiet, alone, 0)
+    for c in norm_copies:
+        c.wait()
+    norm_all[flat, 0, 0:share] = norm_a[...] + norm_b[...]
+    norm_all[flat] = pltpu.roll(norm_all[flat], lax.rem(flat * share, LANES), axis=1)
+    pl.semaphore_wait(barrier, n - 1)
+    early = pl.ds(0, quiet)
+    for i, peer in enumerate(peers):
+        pltpu.make_async_remote_copy(
+            src_ref=part.at[early], dst_ref=part_in.at[me, early],
+            send_sem=part_send.at[i], recv_sem=early_recv.at[me],
+            device_id={"zero": peer}, device_id_type=MESH,
+        ).start()
+
+    def send_norm(d, carry):
+        pltpu.make_async_remote_copy(
+            src_ref=norm_all.at[flat], dst_ref=norm_all.at[flat],
+            send_sem=norm_send, recv_sem=norm_recv,
+            device_id=target(d), device_id_type=MESH,
+        ).start()
+        return carry
+
+    lax.fori_loop(1, n, send_norm, 0)
+    for peer in peers:
+        pltpu.make_async_copy(part_in.at[peer, early], part_in.at[peer, early], early_recv.at[peer]).wait()
+    lax.fori_loop(0, quiet - lag, catch_up, 0)
+    lax.fori_loop(2 * quiet - lag, T, steady, 0)
     columns(gate)
-    run(nb + lag, T, up, up)
-    run(T, T + lag, None, up)
-    columns(up)
-
-    for i, peer in enumerate(peers):
-        pltpu.make_async_copy(part, part, part_send.at[i]).wait()
-        theirs = pl.ds(pl.multiple_of(peer * width, LANES), width)
-        for half, ready in enumerate((ready_g, ready_u)):
-            pltpu.make_async_copy(ready.at[:, mine], ready.at[:, mine], ready_send.at[half, i]).wait()
-            pltpu.make_async_copy(ready.at[:, theirs], ready.at[:, theirs], ready_recv.at[half, peer]).wait()
     others = norm_all.at[pl.ds(0, n - 1)]
     pltpu.make_async_copy(others, others, norm_send).wait()
     pltpu.make_async_copy(others, others, norm_recv).wait()
@@ -176,11 +216,21 @@
         first = d * share // LANES * LANES
         norm_sum[:, first:first + window] += norm_all[d]
     serve_norm[...] = norm_sum[0, :n * share].astype(jnp.bfloat16)
+    lax.fori_loop(T - lag, T, last, 0)
+    columns(up)
+
+    for i, peer in enumerate(peers):
+        pltpu.make_async_copy(part, part, part_send.at[i]).wait()
+        theirs = pl.ds(pl.multiple_of(peer * width, LANES), width)
+        for half, ready in enumerate((ready_g, ready_u)):
+            pltpu.make_async_copy(ready.at[:, mine], ready.at[:, mine], ready_send.at[half, i]).wait()
+            pltpu.make_async_copy(ready.at[:, theirs], ready.at[:, theirs], ready_recv.at[half, peer]).wait()
 
 
 def copy_kernel(*refs):
-    sems = refs[8]
-    copies = [pltpu.make_async_copy(refs[i], refs[4 + i], sems.at[i]) for i in range(4)]
+    count = len(refs) // 2
+    sems = refs[-1]
+    copies = [pltpu.make_async_copy(refs[i], refs[count + i], sems.at[i]) for i in range(count)]
     for c in copies:
         c.start()
     for c in copies:
@@ -195,11 +245,12 @@
     T = 2 * rows // K
     slots = min(8, T)
     lag = 2
+    quiet = max(lag, min(14, (T + lag) // 2))
     window = -(-(share + LANES - 1) // LANES) * LANES
     hbm = pl.BlockSpec(memory_space=pl.ANY)
     vmem = pl.BlockSpec(memory_space=pltpu.VMEM)
     ready_g, ready_u, column_g, column_u, latest_g, latest_u, serve_norm = pl.pallas_call(
-        functools.partial(update_kernel, nz, nm, K, slots, lag),
+        functools.partial(update_kernel, nz, nm, K, slots, lag, quiet),
         out_shape=(
             pltpu.VMEM((rows, nz * width), jnp.bfloat16),
             pltpu.VMEM((rows, nz * width), jnp.bfloat16),
@@ -209,16 +260,18 @@
             pltpu.VMEM((rows, width), jnp.float32),
             pltpu.VMEM((n * share,), jnp.bfloat16),
         ),
-        in_specs=[hbm] * 6 + [vmem] * 2,
+        in_specs=[hbm] * 6 + [pl.BlockSpec(memory_space=pltpu.HBM)] * 2,
         out_specs=(vmem,) * 7,
         scratch_shapes=[
             pltpu.VMEM((slots, K, width), jnp.float32),
             pltpu.VMEM((slots, K, width), jnp.float32),
             pltpu.VMEM((T, K, LANES), jnp.float32),
             pltpu.VMEM((nz, T, K, LANES), jnp.float32),
-            pltpu.VMEM((rows, LANES), jnp.float32),
+            pltpu.VMEM((2 * rows, LANES), jnp.float32),
             pltpu.VMEM((n, 1, window), jnp.float32),
             pltpu.VMEM((1, n * share + window), jnp.float32),
+            pltpu.VMEM((share,), jnp.float32),
+            pltpu.VMEM((share,), jnp.float32),
             pltpu.SemaphoreType.DMA((slots,)),
             pltpu.SemaphoreType.DMA((slots,)),
             pltpu.SemaphoreType.DMA((slots,)),
@@ -228,21 +281,26 @@
             pltpu.SemaphoreType.DMA((2, nz)),
             pltpu.SemaphoreType.DMA,
             pltpu.SemaphoreType.DMA,
+            pltpu.SemaphoreType.DMA((nz,)),
+            pltpu.SemaphoreType.DMA((2,)),
         ],
         compiler_params=pltpu.CompilerParams(
             collective_id=0, has_side_effects=True, vmem_limit_bytes=12 * 1024 * 1024
         ),
         name="update",
-    )(w_gate.T, first_gate.T, second_gate.T, w_up.T, first_up.T, second_up.T, norm_train, norm_step)
-    ready_g, ready_u, latest_g, latest_u = pl.pallas_call(
+    )(w_gate.T, first_gate.T, second_gate.T, w_up.T, first_up.T, second_up.T, *(
+        pltpu.with_memory_space_constraint(x, pltpu.HBM) for x in (norm_train, norm_step)
+    ))
+    results = (ready_g, ready_u, column_g, column_u, latest_g, latest_u, serve_norm)
+    ready_g, ready_u, column_g, column_u, latest_g, latest_u, serve_norm = pl.pallas_call(
         copy_kernel,
-        out_shape=tuple(jax.ShapeDtypeStruct(x.shape, x.dtype) for x in (ready_g, ready_u, latest_g, latest_u)),
-        in_specs=[hbm] * 4,
-        out_specs=(hbm,) * 4,
-        scratch_shapes=[pltpu.SemaphoreType.DMA((4,))],
+        out_shape=tuple(jax.ShapeDtypeStruct(x.shape, x.dtype) for x in results),
+        in_specs=[hbm] * 7,
+        out_specs=(hbm,) * 7,
+        scratch_shapes=[pltpu.SemaphoreType.DMA((7,))],
         compiler_params=pltpu.CompilerParams(vmem_limit_bytes=1024 * 1024),
         name="write",
-    )(ready_g, ready_u, latest_g, latest_u)
+    )(*results)
     return (ready_g.T, ready_u.T, column_g, column_u, serve_norm, latest_g.T, latest_u.T)
 
 

time: 43.1 us -> 38.1 us (0.88)
  local copies, waits for them, and re-layouts: 3.14 us -> 0 us
  Pallas kernels: 39.1 us -> 37.2 us
    unnamed x7 -> x0, local copies, waits for them, and re-layouts: 3.14 us -> none
    pallas_call x1, Pallas kernels: 27.3 us -> 25.3 us  [local(): pl.pallas_call(functools.partial(update_kernel, nz, nm, K, slots, lag, qu...]
where the time goes in v3:
time: 38.1 us; the launch traced here: 37.8 us
  Pallas kernels  37.2 us (98%)
  between operations  0.64 us (2%)
    pallas_call x1, Pallas kernels, local(): pl.pallas_call(functools.partial(update_kernel, nz, nm, K, slots, lag, qu...  25.3 us
    pallas_call x1, Pallas kernels, local(): pl.pallas_call(copy_kernel, out_shape=tuple((jax.ShapeDtypeStruct(x.shape...  11.9 us

profile of v3, /device:TPU:0, one launch (start us, length us, event | category | flops | bytes accessed | tf_op | source)
XLA Modules:
  0.0 37.8 jit_solution(3763935682309648465)
XLA Ops:
  0.6 25.3 %update.1 = (bf16[864,5120]{1,0:T(8,128)(2,1)S(1)}, bf16[864,5120]{1,0:T(8,128)(2,1)S(1)}, f32[864]{0:T(1024)S(1)}, f32[864]{0:T(1024)S(1)}, f32[864,2560]{1,0:T...) custom-call(f32[864,2560]{1,0:T(8,128)} %bitcast.10, f32[864,2560]{1,0:T(8,128)} %bitcast.11, ...), custom_call_target="tpu_custom_call" | custom-call | tf_op jit(solution)/shard_map/update/pallas_call | solution.py:252
  26.0 11.9 %write.1 = (bf16[864,5120]{1,0:T(8,128)(2,1)}, bf16[864,5120]{1,0:T(8,128)(2,1)}, f32[864]{0:T(1024)}, f32[864]{0:T(1024)}, f32[864,2560]{1,0:T(8,128)}, /*index=5*/f32[864,2560]{1,0:T(8,128)}, bf16[5120]{0:T(1024)(128)(2,1)}) custom-call(bf16[864,5120]{1,0:T(8,128)(2,1)S(1)} %get-tuple-element.21.refs_0_, bf16[864,5120]{1,0:T(8,128)(2,1)S(1)} %get-tuple-element.22.refs_1_, ...), custom_call_target="tpu_custom_call" | custom-call | tf_op jit(solution)/shard_map/write/pallas_call | solution.py:295

commit v4 on v3

--- a/solution.py
+++ b/solution.py
@@ -245,7 +245,7 @@
     T = 2 * rows // K
     slots = min(8, T)
     lag = 2
-    quiet = max(lag, min(14, (T + lag) // 2))
+    quiet = max(lag, min(6, (T + lag) // 2))
     window = -(-(share + LANES - 1) // LANES) * LANES
     hbm = pl.BlockSpec(memory_space=pl.ANY)
     vmem = pl.BlockSpec(memory_space=pltpu.VMEM)

time: 38.1 us -> 39.1 us (1.026)
  Pallas kernels: 37.2 us -> 38.3 us
    pallas_call x1, Pallas kernels: 25.3 us -> 26.4 us  [local(): pl.pallas_call(functools.partial(update_kernel, nz, nm, K, slots, lag, qu...]
where the time goes in v4:
time: 39.1 us; the launch traced here: 38.9 us
  Pallas kernels  38.3 us (98%)
  between operations  0.64 us (2%)
    pallas_call x1, Pallas kernels, local(): pl.pallas_call(functools.partial(update_kernel, nz, nm, K, slots, lag, qu...  26.4 us
    pallas_call x1, Pallas kernels, local(): pl.pallas_call(copy_kernel, out_shape=tuple((jax.ShapeDtypeStruct(x.shape...  11.9 us

profile of v4, /device:TPU:0, one launch (start us, length us, event | category | flops | bytes accessed | tf_op | source)
XLA Modules:
  0.0 38.9 jit_solution(15620446598119853784)
XLA Ops:
  0.6 26.4 %update.1 = (bf16[864,5120]{1,0:T(8,128)(2,1)S(1)}, bf16[864,5120]{1,0:T(8,128)(2,1)S(1)}, f32[864]{0:T(1024)S(1)}, f32[864]{0:T(1024)S(1)}, f32[864,2560]{1,0:T...) custom-call(f32[864,2560]{1,0:T(8,128)} %bitcast.10, f32[864,2560]{1,0:T(8,128)} %bitcast.11, ...), custom_call_target="tpu_custom_call" | custom-call | tf_op jit(solution)/shard_map/update/pallas_call | solution.py:252
  27.1 11.9 %write.1 = (bf16[864,5120]{1,0:T(8,128)(2,1)}, bf16[864,5120]{1,0:T(8,128)(2,1)}, f32[864]{0:T(1024)}, f32[864]{0:T(1024)}, f32[864,2560]{1,0:T(8,128)}, /*index=5*/f32[864,2560]{1,0:T(8,128)}, bf16[5120]{0:T(1024)(128)(2,1)}) custom-call(bf16[864,5120]{1,0:T(8,128)(2,1)S(1)} %get-tuple-element.21.refs_0_, bf16[864,5120]{1,0:T(8,128)(2,1)S(1)} %get-tuple-element.22.refs_1_, ...), custom_call_target="tpu_custom_call" | custom-call | tf_op jit(solution)/shard_map/write/pallas_call | solution.py:295
